TPU v7x, 128 devices: a whole 4x4x4 slice. The times are simulated.
128 devices in a mesh: dp: 8 (over z, core), mp: 16 (over x, y).
Axes of the slice: x: 4, y: 4, z: 4, core: 2. Of those that a mesh axis runs over, the one named last changes fastest.
Arguments:
- features: bfloat16 [8192, 2048], P('dp'), may hold values from -21 to 21
- rewards: float32 [32, 256], P('dp'), may hold values from -6 to 6
- old_values: float32 [32, 256], P('dp'), may hold values from -6 to 6
- dones: int32 [32, 256], P('dp'), may hold values 0 or 1
- lengths: int32 [32], P('dp'), may hold values from 128 to 256
- proj_weights: bfloat16 [2048, 2, 8192], P(None, None, 'mp'), may hold values from -0.125 to 0.125
- down_weight: bfloat16 [8192, 2048], P('mp'), may hold values from -0.0625 to 0.0625
- value_head: float32 [2048], replicated, may hold values from -0.0078125 to 0.0078125
- master: float32 [2048, 2, 8192], P('dp', None, 'mp'), may hold values from -0.125 to 0.125
- moment: float32 [2048, 2, 8192], P('dp', None, 'mp'), may hold values from -1.035801e-05 to 1.035801e-05
- second: float32 [2048, 2, 8192], P('dp', None, 'mp'), may hold values from 2.9802322e-13 to 2.9802322e-12
Outputs:
- master_new: float32 [2048, 2, 8192], P('dp', None, 'mp')
- moment_new: float32 [2048, 2, 8192], P('dp', None, 'mp')
- second_new: float32 [2048, 2, 8192], P('dp', None, 'mp')
- working: bfloat16 [2048, 2, 8192], P(None, None, 'mp')
- total_loss: float32 [], replicated
All inputs are finite; a program needn't handle non-finite values. No bound on the sum of `dones` on one device may be relied on, other than what follows from the above.
Results may differ from a plain program's by a relative error of at most 0.0011.
Values may be sent and summed in bfloat16 or wider, within the bound.
A program may use at most 128 MiB of HBM per device.

v0:
```python
import functools
import math
import jax
import jax.numpy as jnp
from jax import lax
from jax.sharding import Mesh
from jax.sharding import PartitionSpec as P

DP = ("dp_0", "dp_1")
MP = ("mp_0", "mp_1")
DP_MP = ("dp_0", "dp_1", "mp_0", "mp_1")
GAMMA = 0.99
LAMBDA = 0.95
MAX_NORM = 0.05


def own_block(parts, axes, sequence):
    shape = [lax.axis_size(a) for a in axes]
    parts = parts.reshape(*shape, *parts.shape[1:])
    parts = parts.transpose(*sequence, *range(len(axes), parts.ndim))
    parts = parts.reshape(-1, *parts.shape[len(axes) :])
    for k in sequence:
        parts = lax.psum_scatter(parts, axes[k], scatter_dimension=0, tiled=True)
    return parts[0]


def in_blocks(value, dim, count):
    before, after = (value.shape[:dim], value.shape[dim + 1 :])
    return jnp.moveaxis(value.reshape(*before, count, -1, *after), dim, 0)


def summed_rows(value, axes, sequence, dim):
    count = lax.axis_size(axes)
    return own_block(in_blocks(value, dim, count), axes, sequence)


def one_axis_at_a_time(value, axes):
    return functools.reduce(lax.psum, axes, value)


def gae_targets(rewards, old_values, dones, lengths):
    seq_len = rewards.shape[1]
    keeps = 1.0 - dones.astype(jnp.float32)
    following = jnp.concatenate([old_values[:, 1:], jnp.zeros_like(old_values[:, :1])], axis=1)
    deltas = rewards + GAMMA * following * keeps - old_values
    counted = jnp.cumsum(dones, axis=1) - dones
    places = jnp.arange(seq_len, dtype=jnp.int32)
    spans = places[None, :] - places[:, None]
    linked = (counted[:, :, None] == counted[:, None, :]) & (spans[None] >= 0)
    powers = jnp.exp(jnp.maximum(spans, 0).astype(jnp.float32) * math.log(GAMMA * LAMBDA))
    kernel = jnp.where(linked, powers[None], jnp.zeros((), jnp.float32))
    advantage = jnp.einsum("ats,as->at", kernel, deltas, precision=lax.Precision.HIGHEST)
    targets = (advantage + old_values).reshape(-1)
    mask = (places[None, :] < lengths[:, None]).astype(jnp.float32).reshape(-1)
    return (targets, mask)


def value_loss(features, mixed, targets, mask, value_head, total_tokens):
    stream = features.astype(jnp.float32) + mixed
    norm_factor = lax.rsqrt(jnp.mean(stream * stream, axis=-1) + 1e-05)
    normed = stream * norm_factor[:, None]
    estimate = jnp.dot(normed, value_head, precision=lax.Precision.HIGHEST)
    errors = estimate - targets
    loss_part = jnp.sum(mask * errors * errors) / total_tokens
    coeff = 2.0 * mask * errors / total_tokens
    head_grad = coeff[:, None] * value_head[None, :]
    out_grad = (
        norm_factor[:, None]
        * (head_grad - normed * jnp.mean(head_grad * normed, axis=-1, keepdims=True))
    ).astype(jnp.bfloat16)
    return (loss_part, out_grad)


def contract_rows(left, right):
    return lax.dot_general(
        left, right, (((0,), (0,)), ((), ())), preferred_element_type=jnp.float32
    )


def per_device(
    features,
    rewards,
    old_values,
    dones,
    lengths,
    proj_weights,
    down_weight,
    value_head,
    master,
    moment,
    second,
):
    token_count = features.shape[0]
    model_width = features.shape[1]
    ff_local = down_weight.shape[0]
    data_ways = lax.axis_size(DP)
    model_ways = lax.axis_size(MP)
    total_tokens = token_count * data_ways
    targets, mask = gae_targets(rewards, old_values, dones, lengths)
    both = jnp.dot(
        features,
        proj_weights.reshape(model_width, 2 * ff_local),
        preferred_element_type=jnp.float32,
    )
    both = both.reshape(token_count, 2, ff_local)
    gate_values = both[:, 0, :]
    up_values = both[:, 1, :]
    hidden = (jax.nn.silu(gate_values) * up_values).astype(jnp.bfloat16)
    mixed = lax.psum(
        jnp.dot(hidden, down_weight, preferred_element_type=jnp.float32).astype(jnp.bfloat16), MP
    ).astype(jnp.float32)
    loss_part, out_grad = value_loss(features, mixed, targets, mask, value_head, total_tokens)
    loss_part = loss_part / model_ways
    hidden_grad = jnp.dot(out_grad, down_weight.T, preferred_element_type=jnp.float32)
    gate_sigmoid = jax.nn.sigmoid(gate_values)
    gate_grad = (
        hidden_grad * up_values * gate_sigmoid * (1.0 + gate_values * (1.0 - gate_sigmoid))
    ).astype(jnp.bfloat16)
    up_grad = (hidden_grad * gate_values * gate_sigmoid).astype(jnp.bfloat16)
    both_grad = jnp.stack([gate_grad, up_grad], axis=1).reshape(token_count, 2 * ff_local)
    row_share = model_width // data_ways
    grads = summed_rows(
        contract_rows(features, both_grad).reshape(row_share * lax.axis_size(DP), 2, ff_local),
        DP,
        (1, 0),
        0,
    )
    squares = jnp.sum(grads * grads)
    squared_total, total_loss = (
        one_axis_at_a_time(squares, DP_MP),
        one_axis_at_a_time(loss_part, DP_MP),
    )
    clip = jnp.minimum(1.0, MAX_NORM / (jnp.sqrt(squared_total) + 1e-06))
    clipped = clip * grads
    moment_new = 0.9 * moment + 0.1 * clipped
    second_new = 0.999 * second + 0.001 * clipped * clipped
    first_hat = moment_new / (1.0 - 0.9**10)
    second_hat = second_new / (1.0 - 0.999**10)
    master_new = master - 0.001 * (first_hat / (jnp.sqrt(second_hat) + 1e-08) + 0.1 * master)
    working = lax.all_gather(master_new.astype(jnp.bfloat16), DP, axis=0, tiled=True)
    return (master_new, moment_new, second_new, working, total_loss)


def solution(mesh):
    finer = Mesh(mesh.devices.reshape(4, 2, 4, 4), ("dp_0", "dp_1", "mp_0", "mp_1"))
    return jax.shard_map(
        per_device,
        mesh=finer,
        in_specs=(
            P(DP, None),
            P(DP, None),
            P(DP, None),
            P(DP, None),
            P(DP),
            P(None, None, MP),
            P(MP, None),
            P(),
            P(DP, None, MP),
            P(DP, None, MP),
            P(DP, None, MP),
        ),
        out_specs=(P(DP, None, MP), P(DP, None, MP), P(DP, None, MP), P(None, None, MP), P()),
        check_vma=False,
    )
```

profile of v0, /device:TPU:1, one launch (start us, length us, event | category | flops | bytes accessed | tf_op | source)
XLA Modules:
  0.0 348.5 jit_solution(17223176488133655442)
XLA Ops:
  7.2 5.5 %copy.34 = bf16[256,8,2,512]{3,1,2,0:T(8,128)(2,1)} copy(bf16[256,8,2,512]{3,2,1,0:T(2,128)(2,1)} %bitcast.73) | data formatting | bytes 8388608
  12.8 6.5 %copy.21 = bf16[1024,2048]{1,0:T(8,128)(2,1)} copy(bf16[1024,2048]{0,1:T(8,128)(2,1)} %bitcast.72) | data formatting | bytes 8388608 | tf_op jit(solution)/shard_map/dot_general | solution.py:100
  19.3 7.6 %fusion.6 = f32[1024,2,512]{0,2,1:T(8,128)S(1)} fusion(bf16[2,512,2048]{2,1,0:T(8,128)(2,1)} %bitcast.74, bf16[1024,2048]{1,0:T(8,128)(2,1)} %param.11), kind=kOutput, calls=%fused_computation.10 | convolution fusion | flops 4294967296 | bytes 12582912 | tf_op jit(solution)/shard_map/dot_general | solution.py:100
  26.9 2.0 copy-done.9
  28.9 4.4 %convolution_convert_fusion = bf16[1024,2048]{1,0:T(8,128)(2,1)} fusion(bf16[512,2048]{1,0:T(8,128)(2,1)S(1)} %copy-done, f32[1024,2,512]{0,2,1:T(8,128)S(1)} %fusion.6), kind=kOutput, calls=%fused_computation.14 | convolution fusion | flops 2152726528 | bytes 10485760 | tf_op jit(solution)/shard_map/dot_general | solution.py:110
  37.1 102.5 %all-reduce.7.cloned.1.call-done = bf16[1024,2048]{1,0:T(8,128)(2,1)} async-done(((bf16[1024,2048]{1,0:T(8,128)(2,1)}), bf16[1024,2048]{1,0:T(8,128)(2,1)}) %all-reduce.7.cloned.1.call-update) | async-done | bytes 4194320 | tf_op jit(solution)/shard_map/psum | solution.py:109
  139.7 5.0 %multiply_reduce_fusion = f32[1024]{0:T(1024)S(1)} fusion(bf16[1024,2048]{1,0:T(8,128)(2,1)} %all-reduce.7.cloned.1.call-done, bf16[1024,2048]{1,0:T(8,128)(2,1)} %param.11), kind=kLoop, calls=%fused_computation.5 | loop fusion | flops 10484736 | bytes 8392704 | tf_op jit(solution)/shard_map/reduce_sum | solution.py:60
  145.6 8.1 %fusion.4 = f32[1,1024]{1,0:T(1,128)S(1)} fusion(f32[2048,1]{0,1:T(1,128)S(1)} %bitcast.76, bf16[1024,2048]{1,0:T(8,128)(2,1)S(1)} %copy-done.3, bf16[1024,2048]{1,0:T(8,128)(2,1)S(1)} %copy-done.2, f32[1024]{0:T(1024)S(1)} %add_rsqrt_fusion), kind=kOutput, calls=%fused_computation.8 | convolution fusion | flops 33554432 | bytes 8404992 | tf_op jit(solution)/shard_map/dot_general | solution.py:62
  154.4 2.6 fusion
  156.9 5.4 %fusion.19 = (bf16[1024,1,512]{0,2,1:T(8,128)(2,1)S(1)}, bf16[1024,1,512]{0,2,1:T(8,128)(2,1)S(1)}) fusion(f32[1024,2,512]{0,2,1:T(8,128)S(1)} %copy-done.10, bf16[512,2048]{1,0:T(8,128)(2,1)S(1)} %copy-done, bf16[1024,2048]{1,0:T(8,128)(2,1)S(1)} %copy-done.3, bf16[1024,2048]{1,0:T(8,128)(2,1)S(1)} %copy-done.2, f32[1024]{0:T(1024)S(1)} %broadcast_multiply_fusion, ...), kind=kOutput, calls=%fused_computation.36 | convolution fusion | flops 2173173760 | bytes 16797696 | tf_op jit(solution)/shard_map/dot_general | solution.py:114
  162.6 6.7 %convolution_bitcast_fusion = f32[2048,1024]{0,1:T(8,128)} fusion(bf16[1024,1024]{0,1:T(8,128)(2,1)S(1)} %bitcast.75, bf16[1024,2048]{1,0:T(8,128)(2,1)S(1)} %copy-done.2), kind=kOutput, calls=%fused_computation.9 | convolution fusion | flops 4294967296 | bytes 14680064 | tf_op jit(solution)/shard_map/dot_general | solution.py:75
  169.3 11.7 %reshape_reshape_reshape.3 = f32[4,2,256,2,512]{2,1,0,4,3:T(2,128)} reshape(f32[2048,1024]{0,1:T(8,128)} %convolution_bitcast_fusion) | data formatting | bytes 16777216 | tf_op jit(solution)/shard_map/reshape;reshape;reshape | solution.py:19
  181.0 13.1 %copy.24 = f32[2,4,256,2,512]{4,2,3,1,0:T(8,128)} copy(f32[2,4,256,2,512]{2,0,1,4,3:T(2,128)} %bitcast.71) | data formatting | bytes 16777216 | tf_op jit(solution)/shard_map/transpose | solution.py:20
  194.2 19.7 %reduce-scatter.3.cloned.1.call-done = f32[4,256,2,512]{3,1,2,0:T(8,128)} async-done(((f32[8,256,2,512]{3,1,2,0:T(8,128)}), f32[4,256,2,512]{3,1,2,0:T(8,128)}) %reduce-scatter.3.cloned.1.call-update) | async-done | bytes 4194320 | tf_op jit(solution)/shard_map/reduce_scatter | solution.py:23
  214.6 49.8 %reduce-scatter.5.cloned.1.call-done = f32[1,256,2,512]{3,1,2,0:T(8,128)} async-done(((f32[4,256,2,512]{3,1,2,0:T(8,128)}), f32[1,256,2,512]{3,1,2,0:T(8,128)}) %reduce-scatter.5.cloned.1.call-update) | async-done | bytes 1048592 | tf_op jit(solution)/shard_map/reduce_scatter | solution.py:23
  264.4 2.1 multiply_reduce_fusion.1
  266.5 7.1 %all-reduce.3 = (f32[]{:T(128)}, f32[]{:T(128)}) all-reduce(f32[]{:T(128)} %multiply_reduce_fusion.1, f32[]{:T(128)S(6)} %div.55), channel_id=1, replica_groups=mesh['dp_0'=4,'dp_1'=2,'mp_0'=4,'mp_1'=4] {'dp_0'}, use_global_device_ids=true, to_apply=%region_8.9 | all-reduce | flops 2 | bytes 16 | tf_op jit(solution)/shard_map/psum | solution.py:38
  273.6 5.5 %all-reduce.4 = (f32[]{:T(128)}, f32[]{:T(128)}) all-reduce(f32[]{:T(128)} %get-tuple-element.14, f32[]{:T(128)} %get-tuple-element.15), channel_id=1, replica_groups=mesh['dp_0'=4,'dp_1'=2,'mp_0'=4,'mp_1'=4] {'dp_1'}, use_global_device_ids=true, to_apply=%region_9.10 | all-reduce | flops 2 | bytes 16 | tf_op jit(solution)/shard_map/psum | solution.py:38
  279.1 9.0 %all-reduce.2 = (f32[]{:T(128)}, f32[]{:T(128)}) all-reduce(f32[]{:T(128)} %get-tuple-element.16, f32[]{:T(128)} %get-tuple-element.17), channel_id=1, replica_groups=mesh['dp_0'=4,'dp_1'=2,'mp_0'=4,'mp_1'=4] {'mp_0'}, use_global_device_ids=true, to_apply=%region_10.11 | all-reduce | flops 2 | bytes 16 | tf_op jit(solution)/shard_map/psum | solution.py:38
  288.1 9.1 %all-reduce.1 = (f32[]{:T(128)}, f32[]{:T(128)}) all-reduce(f32[]{:T(128)} %get-tuple-element.12, f32[]{:T(128)} %get-tuple-element.13), channel_id=1, replica_groups=mesh['dp_0'=4,'dp_1'=2,'mp_0'=4,'mp_1'=4] {'mp_1'}, use_global_device_ids=true, to_apply=%region_11.12 | all-reduce | flops 2 | bytes 16 | tf_op jit(solution)/shard_map/psum | solution.py:38
  297.9 3.2 fusion.31
  302.5 1.8 copy.29
  307.8 26.3 %all-gather.2.cloned.1.call-done = bf16[2048,2,512]{2,1,0:T(2,128)(2,1)} async-done(((bf16[256,2,512]{2,1,0:T(2,128)(2,1)}), bf16[2048,2,512]{2,1,0:T(2,128)(2,1)}) %all-gather.2.cloned.1.call-update) | async-done | bytes 4194320 | tf_op jit(solution)/shard_map/all_gather | solution.py:140
  334.1 7.8 %copy.53 = bf16[2048,2,512]{2,1,0:T(2,128)(2,1)} copy(bf16[2048,2,512]{2,1,0:T(2,128)(2,1)} %all-gather.2.cloned.1.call-done) | data formatting | bytes 8388608
  (54 shorter events, 10.5 us)
Async XLA Ops:
  7.2 21.7 %copy-start = (bf16[512,2048]{1,0:T(8,128)(2,1)S(1)}, bf16[512,2048]{1,0:T(8,128)(2,1)}, u32[]{:S(2)}) copy-start(bf16[512,2048]{1,0:T(8,128)(2,1)} %param.17) | copy-start | bytes 6291460
  7.2 132.5 %all-reduce.7.cloned.1.call-start = ((), (), s32[]{:S(2)}) async-start(), calls=%async_computation.2 | async-start | bytes 8388608 | tf_op jit(solution)/shard_map/psum | solution.py:109
  26.9 2.0 copy-start.9
  33.3 0.7 copy-start.8
  33.3 0.7 copy-start.5
  33.3 0.8 copy-start.4
  33.3 2.5 copy-start.7
  33.4 180.5 %reduce-scatter.3.cloned.1.call-start = ((), (), s32[]{:S(2)}) async-start(), calls=%async_computation.3 | async-start | bytes 12582912 | tf_op jit(solution)/shard_map/reduce_scatter | solution.py:23
  37.1 107.6 %copy-start.6 = (f32[2048]{0:T(1024)S(1)}, f32[2048]{0:T(1024)}, u32[]{:S(2)}) copy-start(f32[2048]{0:T(1024)} %param.18) | copy-start | bytes 24580
  139.7 5.1 %copy-start.2 = (bf16[1024,2048]{1,0:T(8,128)(2,1)S(1)}, bf16[1024,2048]{1,0:T(8,128)(2,1)}, u32[]{:S(2)}) copy-start(bf16[1024,2048]{1,0:T(8,128)(2,1)} %param.11) | copy-start | bytes 12582916
  139.7 5.9 %copy-start.3 = (bf16[1024,2048]{1,0:T(8,128)(2,1)S(1)}, bf16[1024,2048]{1,0:T(8,128)(2,1)}, u32[]{:S(2)}) copy-start(bf16[1024,2048]{1,0:T(8,128)(2,1)} %all-reduce.7.cloned.1.call-done) | copy-start | bytes 12582916
  154.3 2.6 copy-start.10
  194.1 70.3 %reduce-scatter.5.cloned.1.call-start = ((), (), s32[]{:S(2)}) async-start(), calls=%async_computation.4 | async-start | bytes 5242880 | tf_op jit(solution)/shard_map/reduce_scatter | solution.py:23
  213.9 120.2 %all-gather.2.cloned.1.call-start = ((), (), s32[]{:S(2)}) async-start(), calls=%async_computation.5 | async-start | bytes 4718592 | tf_op jit(solution)/shard_map/all_gather | solution.py:140
  334.1 7.9 %copy-start.1 = (bf16[512,2048]{1,0:T(8,128)(2,1)S(1)}, bf16[512,2048]{1,0:T(8,128)(2,1)}, u32[]{:S(2)}) copy-start(bf16[512,2048]{1,0:T(8,128)(2,1)} %param.17) | copy-start | bytes 6291460
Sparse Core Ops, SparseCore 0:
  33.5 106.1 all-reduce.6
  194.2 19.5 reduce-scatter.2
  216.3 48.0 reduce-scatter.4
  302.6 31.4 all-gather.1
where the time goes:
time: 350 us; the launch traced here: 348 us
  waiting for transfers between devices  198 us (57%)
  local copies, waits for them, and re-layouts  55.1 us (16%)
  matrix products  33.5 us (10%)
  blocking collectives  30.7 us (9%)
  other arithmetic  15.3 us (4%)
  between operations  15.3 us (4%)
    psum x1, waiting for transfers between devices, per_device(): lax.psum(jnp.dot(hidden, down_weight, preferred_element_type=jnp.float32)...  103 us
    reduce_scatter x2, waiting for transfers between devices, own_block(): parts = lax.psum_scatter(parts, axes[k], scatter_dimension=0, tiled=True)  69.5 us
    psum x4, blocking collectives, one_axis_at_a_time(): return functools.reduce(lax.psum, axes, value)  30.7 us
    all_gather x1, waiting for transfers between devices, per_device(): lax.all_gather(master_new.astype(jnp.bfloat16), DP, axis=0, tiled=True)  26.3 us
    unnamed x28, local copies, waits for them, and re-layouts  22 us
    transpose x1, local copies, waits for them, and re-layouts, own_block(): parts = parts.transpose(*sequence, *range(len(axes), parts.ndim))  13.1 us
    another operation x1, local copies, waits for them, and re-layouts, own_block(): parts = parts.reshape(*shape, *parts.shape[1:])  11.7 us
    dot_general x1, matrix products, value_loss(): estimate = jnp.dot(normed, value_head, precision=lax.Precision.HIGHEST)  8.13 us
  transfers between devices with their start and end apart: 4, of which 4 were waited for; matrix products, arithmetic and copies ran while one was open for 2% of the time, Pallas kernels for 0%

commit v1 on v0

--- a/solution.py
+++ b/solution.py
@@ -12,6 +12,11 @@
 GAMMA = 0.99
 LAMBDA = 0.95
 MAX_NORM = 0.05
+
+
+def one_after_other(value_2, one, other):
+    inner = lax.psum(value_2, one)
+    return lax.psum(inner, other)
 
 
 def own_block(parts, axes, sequence):
@@ -106,8 +111,10 @@
     gate_values = both[:, 0, :]
     up_values = both[:, 1, :]
     hidden = (jax.nn.silu(gate_values) * up_values).astype(jnp.bfloat16)
-    mixed = lax.psum(
-        jnp.dot(hidden, down_weight, preferred_element_type=jnp.float32).astype(jnp.bfloat16), MP
+    mixed = one_after_other(
+        jnp.dot(hidden, down_weight, preferred_element_type=jnp.float32).astype(jnp.bfloat16),
+        "mp_1",
+        "mp_0",
     ).astype(jnp.float32)
     loss_part, out_grad = value_loss(features, mixed, targets, mask, value_head, total_tokens)
     loss_part = loss_part / model_ways

time: 350 us -> 434 us (1.24)
  waiting for transfers between devices: 198 us -> 283 us
    psum x1 -> x2, waiting for transfers between devices: 103 us -> 187 us  [the longest x1 95.9 us: one_after_other(): inner = lax.psum(value_2, one)]
  transfers between devices with their start and end apart: 4 -> 5, of which waited for: 4 -> 5; matrix products, arithmetic and copies ran while one was open for 2% -> 2% of each run, Pallas kernels for 0% -> 0%
where the time goes in v1:
time: 434 us; the launch traced here: 433 us
  waiting for transfers between devices  283 us (65%)
  local copies, waits for them, and re-layouts  54.7 us (13%)
  matrix products  33.5 us (8%)
  blocking collectives  30.7 us (7%)
  other arithmetic  15.3 us (4%)
  between operations  15.3 us (4%)
    psum x1, waiting for transfers between devices, one_after_other(): inner = lax.psum(value_2, one)  95.9 us
    psum x1, waiting for transfers between devices, one_after_other(): return lax.psum(inner, other)  91.5 us
    reduce_scatter x2, waiting for transfers between devices, own_block(): parts = lax.psum_scatter(parts, axes[k], scatter_dimension=0, tiled=True)  69.3 us
    psum x4, blocking collectives, one_axis_at_a_time(): return functools.reduce(lax.psum, axes, value)  30.7 us
    all_gather x1, waiting for transfers between devices, per_device(): lax.all_gather(master_new.astype(jnp.bfloat16), DP, axis=0, tiled=True)  26.3 us
    unnamed x28, local copies, waits for them, and re-layouts  21.6 us
    transpose x1, local copies, waits for them, and re-layouts, own_block(): parts = parts.transpose(*sequence, *range(len(axes), parts.ndim))  13.1 us
    another operation x1, local copies, waits for them, and re-layouts, own_block(): parts = parts.reshape(*shape, *parts.shape[1:])  11.7 us
  transfers between devices with their start and end apart: 5, of which 5 were waited for; matrix products, arithmetic and copies ran while one was open for 2% of the time, Pallas kernels for 0%

profile of v1, /device:TPU:1, one launch (start us, length us, event | category | flops | bytes accessed | tf_op | source)
XLA Modules:
  0.0 432.8 jit_solution(13909013748216045495)
XLA Ops:
  7.2 5.5 %copy.34 = bf16[256,8,2,512]{3,1,2,0:T(8,128)(2,1)} copy(bf16[256,8,2,512]{3,2,1,0:T(2,128)(2,1)} %bitcast.73) | data formatting | bytes 8388608
  12.8 6.5 %copy.21 = bf16[1024,2048]{1,0:T(8,128)(2,1)} copy(bf16[1024,2048]{0,1:T(8,128)(2,1)} %bitcast.72) | data formatting | bytes 8388608 | tf_op jit(solution)/shard_map/dot_general | solution.py:105
  19.3 7.6 %fusion.6 = f32[1024,2,512]{0,2,1:T(8,128)S(1)} fusion(bf16[2,512,2048]{2,1,0:T(8,128)(2,1)} %bitcast.74, bf16[1024,2048]{1,0:T(8,128)(2,1)} %param.11), kind=kOutput, calls=%fused_computation.10 | convolution fusion | flops 4294967296 | bytes 12582912 | tf_op jit(solution)/shard_map/dot_general | solution.py:105
  26.9 2.0 copy-done.9
  28.9 4.4 %convolution_convert_fusion = bf16[1024,2048]{1,0:T(8,128)(2,1)} fusion(bf16[512,2048]{1,0:T(8,128)(2,1)S(1)} %copy-done, f32[1024,2,512]{0,2,1:T(8,128)S(1)} %fusion.6), kind=kOutput, calls=%fused_computation.14 | convolution fusion | flops 2152726528 | bytes 10485760 | tf_op jit(solution)/shard_map/dot_general | solution.py:115
  33.4 95.9 %all-reduce.8.cloned.1.call-done = bf16[1024,2048]{1,0:T(8,128)(2,1)} async-done(((bf16[1024,2048]{1,0:T(8,128)(2,1)}), bf16[1024,2048]{1,0:T(8,128)(2,1)}) %all-reduce.8.cloned.1.call-update) | async-done | bytes 4194320 | tf_op jit(solution)/shard_map/psum | solution.py:18
  132.7 91.5 %all-reduce.10.cloned.1.call-done = bf16[1024,2048]{1,0:T(8,128)(2,1)} async-done(((bf16[1024,2048]{1,0:T(8,128)(2,1)}), bf16[1024,2048]{1,0:T(8,128)(2,1)}) %all-reduce.10.cloned.1.call-update) | async-done | bytes 4194320 | tf_op jit(solution)/shard_map/psum | solution.py:19
  224.3 5.0 %multiply_reduce_fusion = f32[1024]{0:T(1024)S(1)} fusion(bf16[1024,2048]{1,0:T(8,128)(2,1)} %all-reduce.10.cloned.1.call-done, bf16[1024,2048]{1,0:T(8,128)(2,1)} %param.11), kind=kLoop, calls=%fused_computation.5 | loop fusion | flops 10484736 | bytes 8392704 | tf_op jit(solution)/shard_map/reduce_sum | solution.py:65
  230.2 8.1 %fusion.4 = f32[1,1024]{1,0:T(1,128)S(1)} fusion(f32[2048,1]{0,1:T(1,128)S(1)} %bitcast.76, bf16[1024,2048]{1,0:T(8,128)(2,1)S(1)} %copy-done.3, bf16[1024,2048]{1,0:T(8,128)(2,1)S(1)} %copy-done.2, f32[1024]{0:T(1024)S(1)} %add_rsqrt_fusion), kind=kOutput, calls=%fused_computation.8 | convolution fusion | flops 33554432 | bytes 8404992 | tf_op jit(solution)/shard_map/dot_general | solution.py:67
  238.9 2.6 fusion
  241.5 5.4 %fusion.19 = (bf16[1024,1,512]{0,2,1:T(8,128)(2,1)S(1)}, bf16[1024,1,512]{0,2,1:T(8,128)(2,1)S(1)}) fusion(f32[1024,2,512]{0,2,1:T(8,128)S(1)} %copy-done.10, bf16[512,2048]{1,0:T(8,128)(2,1)S(1)} %copy-done, bf16[1024,2048]{1,0:T(8,128)(2,1)S(1)} %copy-done.3, bf16[1024,2048]{1,0:T(8,128)(2,1)S(1)} %copy-done.2, f32[1024]{0:T(1024)S(1)} %broadcast_multiply_fusion, ...), kind=kOutput, calls=%fused_computation.36 | convolution fusion | flops 2173173760 | bytes 16797696 | tf_op jit(solution)/shard_map/dot_general | solution.py:121
  247.2 6.7 %convolution_bitcast_fusion = f32[2048,1024]{0,1:T(8,128)} fusion(bf16[1024,1024]{0,1:T(8,128)(2,1)S(1)} %bitcast.75, bf16[1024,2048]{1,0:T(8,128)(2,1)S(1)} %copy-done.2), kind=kOutput, calls=%fused_computation.9 | convolution fusion | flops 4294967296 | bytes 14680064 | tf_op jit(solution)/shard_map/dot_general | solution.py:80
  253.9 11.7 %reshape_reshape_reshape.3 = f32[4,2,256,2,512]{2,1,0,4,3:T(2,128)} reshape(f32[2048,1024]{0,1:T(8,128)} %convolution_bitcast_fusion) | data formatting | bytes 16777216 | tf_op jit(solution)/shard_map/reshape;reshape;reshape | solution.py:24
  265.6 13.1 %copy.24 = f32[2,4,256,2,512]{4,2,3,1,0:T(8,128)} copy(f32[2,4,256,2,512]{2,0,1,4,3:T(2,128)} %bitcast.71) | data formatting | bytes 16777216 | tf_op jit(solution)/shard_map/transpose | solution.py:25
  278.8 19.6 %reduce-scatter.3.cloned.1.call-done = f32[4,256,2,512]{3,1,2,0:T(8,128)} async-done(((f32[8,256,2,512]{3,1,2,0:T(8,128)}), f32[4,256,2,512]{3,1,2,0:T(8,128)}) %reduce-scatter.3.cloned.1.call-update) | async-done | bytes 4194320 | tf_op jit(solution)/shard_map/reduce_scatter | solution.py:28
  299.1 49.6 %reduce-scatter.5.cloned.1.call-done = f32[1,256,2,512]{3,1,2,0:T(8,128)} async-done(((f32[4,256,2,512]{3,1,2,0:T(8,128)}), f32[1,256,2,512]{3,1,2,0:T(8,128)}) %reduce-scatter.5.cloned.1.call-update) | async-done | bytes 1048592 | tf_op jit(solution)/shard_map/reduce_scatter | solution.py:28
  348.7 2.1 multiply_reduce_fusion.1
  350.8 7.1 %all-reduce.3 = (f32[]{:T(128)}, f32[]{:T(128)}) all-reduce(f32[]{:T(128)} %multiply_reduce_fusion.1, f32[]{:T(128)S(6)} %div.55), channel_id=1, replica_groups=mesh['dp_0'=4,'dp_1'=2,'mp_0'=4,'mp_1'=4] {'dp_0'}, use_global_device_ids=true, to_apply=%region_9.10 | all-reduce | flops 2 | bytes 16 | tf_op jit(solution)/shard_map/psum | solution.py:43
  357.9 5.5 %all-reduce.4 = (f32[]{:T(128)}, f32[]{:T(128)}) all-reduce(f32[]{:T(128)} %get-tuple-element.14, f32[]{:T(128)} %get-tuple-element.15), channel_id=1, replica_groups=mesh['dp_0'=4,'dp_1'=2,'mp_0'=4,'mp_1'=4] {'dp_1'}, use_global_device_ids=true, to_apply=%region_10.11 | all-reduce | flops 2 | bytes 16 | tf_op jit(solution)/shard_map/psum | solution.py:43
  363.4 9.0 %all-reduce.2 = (f32[]{:T(128)}, f32[]{:T(128)}) all-reduce(f32[]{:T(128)} %get-tuple-element.16, f32[]{:T(128)} %get-tuple-element.17), channel_id=1, replica_groups=mesh['dp_0'=4,'dp_1'=2,'mp_0'=4,'mp_1'=4] {'mp_0'}, use_global_device_ids=true, to_apply=%region_11.12 | all-reduce | flops 2 | bytes 16 | tf_op jit(solution)/shard_map/psum | solution.py:43
  372.4 9.1 %all-reduce.1 = (f32[]{:T(128)}, f32[]{:T(128)}) all-reduce(f32[]{:T(128)} %get-tuple-element.12, f32[]{:T(128)} %get-tuple-element.13), channel_id=1, replica_groups=mesh['dp_0'=4,'dp_1'=2,'mp_0'=4,'mp_1'=4] {'mp_1'}, use_global_device_ids=true, to_apply=%region_12.13 | all-reduce | flops 2 | bytes 16 | tf_op jit(solution)/shard_map/psum | solution.py:43
  382.2 3.2 fusion.31
  392.2 26.3 %all-gather.2.cloned.1.call-done = bf16[2048,2,512]{2,1,0:T(2,128)(2,1)} async-done(((bf16[256,2,512]{2,1,0:T(2,128)(2,1)}), bf16[2048,2,512]{2,1,0:T(2,128)(2,1)}) %all-gather.2.cloned.1.call-update) | async-done | bytes 4194320 | tf_op jit(solution)/shard_map/all_gather | solution.py:147
  418.4 7.8 %copy.54 = bf16[2048,2,512]{2,1,0:T(2,128)(2,1)} copy(bf16[2048,2,512]{2,1,0:T(2,128)(2,1)} %all-gather.2.cloned.1.call-done) | data formatting | bytes 8388608
  (57 shorter events, 12.0 us)
Async XLA Ops:
  7.2 21.7 %copy-start = (bf16[512,2048]{1,0:T(8,128)(2,1)S(1)}, bf16[512,2048]{1,0:T(8,128)(2,1)}, u32[]{:S(2)}) copy-start(bf16[512,2048]{1,0:T(8,128)(2,1)} %param.17) | copy-start | bytes 6291460
  7.2 122.1 %all-reduce.8.cloned.1.call-start = ((), (), s32[]{:S(2)}) async-start(), calls=%async_computation.2 | async-start | bytes 8388608 | tf_op jit(solution)/shard_map/psum | solution.py:18
  26.9 2.0 copy-start.9
  33.3 96.2 %copy-start.8 = (s32[4]{0:T(128)S(1)}, s32[4]{0:T(128)}, u32[]{:S(2)}) copy-start(s32[4]{0:T(128)} %param.15) | copy-start | bytes 52
  33.3 96.3 %copy-start.5 = (f32[4,256]{1,0:T(4,128)S(1)}, f32[4,256]{1,0:T(4,128)}, u32[]{:S(2)}) copy-start(f32[4,256]{1,0:T(4,128)} %param.13) | copy-start | bytes 12292
  33.3 96.4 %copy-start.4 = (s32[4,256]{1,0:T(4,128)S(1)}, s32[4,256]{1,0:T(4,128)}, u32[]{:S(2)}) copy-start(s32[4,256]{1,0:T(4,128)} %param.14) | copy-start | bytes 12292
  33.3 98.1 %copy-start.7 = (f32[4,256]{1,0:T(4,128)S(1)}, f32[4,256]{1,0:T(4,128)}, u32[]{:S(2)}) copy-start(f32[4,256]{1,0:T(4,128)} %param.12) | copy-start | bytes 12292
  33.4 190.9 %all-reduce.10.cloned.1.call-start = ((), (), s32[]{:S(2)}) async-start(), calls=%async_computation.3 | async-start | bytes 8388608 | tf_op jit(solution)/shard_map/psum | solution.py:19
  129.3 169.1 %reduce-scatter.3.cloned.1.call-start = ((), (), s32[]{:S(2)}) async-start(), calls=%async_computation.4 | async-start | bytes 12582912 | tf_op jit(solution)/shard_map/reduce_scatter | solution.py:28
  132.7 96.6 %copy-start.6 = (f32[2048]{0:T(1024)S(1)}, f32[2048]{0:T(1024)}, u32[]{:S(2)}) copy-start(f32[2048]{0:T(1024)} %param.18) | copy-start | bytes 24580
  224.3 5.1 %copy-start.2 = (bf16[1024,2048]{1,0:T(8,128)(2,1)S(1)}, bf16[1024,2048]{1,0:T(8,128)(2,1)}, u32[]{:S(2)}) copy-start(bf16[1024,2048]{1,0:T(8,128)(2,1)} %param.11) | copy-start | bytes 12582916
  224.3 5.9 %copy-start.3 = (bf16[1024,2048]{1,0:T(8,128)(2,1)S(1)}, bf16[1024,2048]{1,0:T(8,128)(2,1)}, u32[]{:S(2)}) copy-start(bf16[1024,2048]{1,0:T(8,128)(2,1)} %all-reduce.10.cloned.1.call-done) | copy-start | bytes 12582916
  238.9 2.6 copy-start.10
  278.7 70.0 %reduce-scatter.5.cloned.1.call-start = ((), (), s32[]{:S(2)}) async-start(), calls=%async_computation.5 | async-start | bytes 5242880 | tf_op jit(solution)/shard_map/reduce_scatter | solution.py:28
  298.4 120.0 %all-gather.2.cloned.1.call-start = ((), (), s32[]{:S(2)}) async-start(), calls=%async_computation.6 | async-start | bytes 4718592 | tf_op jit(solution)/shard_map/all_gather | solution.py:147
  418.4 7.9 %copy-start.1 = (bf16[512,2048]{1,0:T(8,128)(2,1)S(1)}, bf16[512,2048]{1,0:T(8,128)(2,1)}, u32[]{:S(2)}) copy-start(bf16[512,2048]{1,0:T(8,128)(2,1)} %param.17) | copy-start | bytes 6291460
Sparse Core Ops, SparseCore 0:
  33.5 95.7 all-reduce.7
  131.7 92.5 all-reduce.9
  278.8 19.5 reduce-scatter.2
  300.7 48.0 reduce-scatter.4
  386.9 31.4 all-gather.1
